TPU v7x, 32 devices: a whole 2x2x4 slice. The times are simulated.
32 devices in a mesh: tm: 4 (over y, x), space: 8 (over z, core).
Axes of the slice: x: 2, y: 2, z: 4, core: 2. Of those that a mesh axis runs over, the one named last changes fastest.
Arguments:
- residual: float32 [64, 64, 8, 128], P('tm', 'space'), may hold values from -24 to 24
- capacity: float32 [64, 8, 128], P('space'), may hold values from 0.25 to 4
Outputs:
- preconditioned: float32 [64, 64, 8, 128], P('tm', 'space')
All inputs are finite; a program needn't handle non-finite values.
Results may differ from a plain program's by a relative error of at most 0.0003.
Values sent between devices are 32-bit elements; how exact they have to be, the bound alone decides.
A program may use at most 64 MiB of HBM per device.

v0:
```python
import functools
import math

import jax
import jax.numpy as jnp
import numpy as np
from jax import lax
from jax.experimental import pallas as pl
from jax.experimental.pallas import tpu as pltpu
from jax.sharding import PartitionSpec as P

GRID_DEPTH = 4
SMOOTH = 2
COARSE_SWEEPS = 6


ALPHA_CORNER = 0.01
STEP_SIZE = 0.5
DIFFUSE = 2.0
ADVECT = (0.2, -0.15, 0.1)
OMEGA = 0.7
HIGHEST = lax.Precision.HIGHEST


def extended(array, sides, width):
    for axis, dim in sides:
        peers, length = (lax.axis_size(axis), array.shape[dim])
        up = [(i, (i + 1) % peers) for i in range(peers - 1)]
        down = [(j, i) for i, j in up]
        last = lax.slice_in_dim(array, length - width, length, axis=dim)
        initial = lax.slice_in_dim(array, 0, width, axis=dim)
        before = lax.ppermute(last, axis, up)
        after = lax.ppermute(initial, axis, down)
        array = jnp.concatenate([before, array, after], axis=dim)
    return array


def level_coefficients(per_level_values):
    spread = DIFFUSE / 4.0**per_level_values
    drifts = tuple((component / 2.0**per_level_values for component in ADVECT))
    return (spread, drifts)


def pad_second(volume, position):
    widths = [(0, 0)] * volume.ndim
    widths[position] = (1, 1)
    return jnp.pad(volume, widths)


def apply_operator(padded, current_capacity, spectral_shifts, per_level_values):
    spread, drifts = level_coefficients(per_level_values)
    centre = padded[:, :, 1:-1]
    upper_first = padded[:, :, 2:]
    lower_first = padded[:, :, :-2]
    wide_second = pad_second(centre, 3)
    upper_second = wide_second[:, :, :, 2:]
    lower_second = wide_second[:, :, :, :-2]
    wide_third = pad_second(centre, 4)
    upper_third = wide_third[:, :, :, :, 2:]
    lower_third = wide_third[:, :, :, :, :-2]
    stencil = spread * (
        6.0 * centre
        - upper_first
        - lower_first
        - upper_second
        - lower_second
        - upper_third
        - lower_third
    )
    stencil = (
        stencil
        + drifts[0] * (upper_first - lower_first)
        + drifts[1] * (upper_second - lower_second)
        + drifts[2] * (upper_third - lower_third)
    )
    first_shift, second_shift, third_shift = spectral_shifts
    real_part = centre[0]
    imag_part = centre[1]
    shifted = jnp.stack(
        [
            current_capacity * (first_shift * real_part - second_shift * imag_part),
            current_capacity * (second_shift * real_part + third_shift * imag_part),
        ]
    )
    return stencil + shifted


def inverse_diagonal(current_capacity, spectral_shifts, per_level_values):
    spread, drifts = level_coefficients(per_level_values)
    first_shift, second_shift, third_shift = spectral_shifts
    top_left = current_capacity * first_shift + 6.0 * spread
    coupling = current_capacity * second_shift
    bottom_right = current_capacity * third_shift + 6.0 * spread
    determinant = top_left * bottom_right + coupling * coupling
    return (bottom_right / determinant, coupling / determinant, top_left / determinant)


def damped_update(residual_now, inverse):
    diagonal_a, diagonal_b, diagonal_c = inverse
    return OMEGA * jnp.stack(
        [
            diagonal_a * residual_now[0] + diagonal_b * residual_now[1],
            diagonal_c * residual_now[1] - diagonal_b * residual_now[0],
        ]
    )


def restrict_to_coarse(volume):
    leading = volume.shape[:-3]
    first_extent, second_extent, third_extent = volume.shape[-3:]
    blocks = volume.reshape(
        leading + (first_extent // 2, 2, second_extent // 2, 2, third_extent // 2, 2)
    )
    lead_count = len(leading)
    return jnp.mean(blocks, axis=(lead_count + 1, lead_count + 3, lead_count + 5))


def prolong_cells(volume):
    leading = volume.shape[:-3]
    first_extent, second_extent, third_extent = volume.shape[-3:]
    expanded = jnp.broadcast_to(
        volume[..., :, None, :, None, :, None],
        leading + (first_extent, 2, second_extent, 2, third_extent, 2),
    )
    return expanded.reshape(leading + (2 * first_extent, 2 * second_extent, 2 * third_extent))


def shift_values(frequency, length):
    ratio_step = ALPHA_CORNER ** (1.0 / length)
    phases = 2.0 * math.pi / length * frequency.astype(jnp.float32)
    first_shift = (1.0 - ratio_step * jnp.cos(phases)) / STEP_SIZE
    second_shift = ratio_step * jnp.sin(phases) / STEP_SIZE
    leading = frequency == 0
    second_shift = jnp.where(leading, 0.0, second_shift)
    third_shift = jnp.where(leading, (1.0 + ratio_step) / STEP_SIZE, first_shift)
    return tuple(
        (column.reshape(-1, 1, 1, 1) for column in (first_shift, second_shift, third_shift))
    )


def phase_grid(row_count, length):
    integers = (
        jnp.arange(row_count, dtype=jnp.int32)[:, None]
        * jnp.arange(length, dtype=jnp.int32)[None, :]
        % length
    )
    return 2.0 * math.pi / length * integers.astype(jnp.float32)


def pad_faces(volume):
    return extended(volume, (("space", 2),), 1)


def multigrid_cycle(
    per_level_values,
    forcing_term,
    capacity_fields,
    spectral_shifts,
    shared_values,
    assemble_level,
    assemble_parts,
):
    current_capacity = capacity_fields[per_level_values]
    inverse = inverse_diagonal(current_capacity, spectral_shifts, per_level_values)
    coarsest = per_level_values == GRID_DEPTH - 1
    current = damped_update(forcing_term, inverse)
    for repeat in range((COARSE_SWEEPS if coarsest else SMOOTH) - 1):
        current = current + damped_update(
            forcing_term
            - apply_operator(
                pad_faces(current), current_capacity, spectral_shifts, per_level_values
            ),
            inverse,
        )
    if coarsest:
        return current
    coarse_right_hand = restrict_to_coarse(
        forcing_term
        - apply_operator(pad_faces(current), current_capacity, spectral_shifts, per_level_values)
    )
    coarse_solution = multigrid_cycle(
        per_level_values + 1,
        coarse_right_hand,
        capacity_fields,
        spectral_shifts,
        shared_values,
        assemble_level,
        assemble_parts,
    )
    current = current + prolong_cells(coarse_solution)
    for repeat in range(SMOOTH):
        current = current + damped_update(
            forcing_term
            - apply_operator(
                pad_faces(current), current_capacity, spectral_shifts, per_level_values
            ),
            inverse,
        )
    return current


def on_device(residual, capacity):
    steps_here, thickness, extent_second, extent_third = residual.shape
    length = lax.axis_size("tm") * steps_here
    ratio_step = ALPHA_CORNER ** (1.0 / length)
    moments = (lax.axis_index("tm") * steps_here + jnp.arange(steps_here, dtype=jnp.int32)).astype(
        jnp.float32
    )
    scaled = (residual * jnp.power(ratio_step, moments)[:, None, None, None]).reshape(
        steps_here, -1
    )
    series = lax.all_to_all(scaled, "tm", split_axis=1, concat_axis=0, tiled=True)
    all_weights = jnp.power(ratio_step, jnp.arange(length, dtype=jnp.float32))
    alternate = 1.0 - 2.0 * (jnp.arange(length, dtype=jnp.int32) % 2).astype(jnp.float32)
    capacity_fields = [capacity]
    for per_level_values in range(1, GRID_DEPTH):
        capacity_fields.append(restrict_to_coarse(capacity_fields[-1]))
    halves = length // 2
    phases = phase_grid(halves, length)
    first_row = jnp.arange(halves, dtype=jnp.int32)[:, None] == 0
    forward = jnp.concatenate(
        [jnp.cos(phases), jnp.where(first_row, alternate[None, :], -jnp.sin(phases))], axis=0
    )
    spectrum = jnp.dot(forward, series, precision=HIGHEST).reshape(2, halves, -1)
    received = lax.all_to_all(spectrum, "tm", split_axis=1, concat_axis=2, tiled=True)
    slot_count = steps_here // 2
    frequency = lax.axis_index("tm") * slot_count + jnp.arange(slot_count, dtype=jnp.int32)
    spectral_shifts = shift_values(frequency, length)
    field_list = received.reshape(2, slot_count, thickness, extent_second, extent_third)
    solved_fields = multigrid_cycle(
        0, field_list, capacity_fields, spectral_shifts, False, GRID_DEPTH, None
    )
    flattened = solved_fields.reshape(2, slot_count, -1)
    returned = lax.all_to_all(flattened, "tm", split_axis=2, concat_axis=1, tiled=True)
    halves = length // 2
    phases = jnp.transpose(phase_grid(halves, length))
    first_column = jnp.arange(halves, dtype=jnp.int32)[None, :] == 0
    real_columns = jnp.where(first_column, 1.0, 2.0 * jnp.cos(phases)) / length
    imag_columns = jnp.where(first_column, alternate[:, None], -2.0 * jnp.sin(phases)) / length
    inverse_table = jnp.concatenate([real_columns, imag_columns], axis=1)
    values = jnp.dot(
        inverse_table,
        returned.reshape(returned.shape[0] * returned.shape[1], -1),
        precision=HIGHEST,
    )
    values = values / all_weights[:, None]
    result = lax.all_to_all(values, "tm", split_axis=0, concat_axis=1, tiled=True)
    return result.reshape(residual.shape)


MESH = pl.DeviceIdType.MESH


def real_transform(values):
    count = len(values)
    if count == 1:
        return [(values[0], None)]
    evens, odds = real_transform(values[0::2]), real_transform(values[1::2])
    half = count // 2
    if count == 2:
        return [(evens[0][0] + odds[0][0], None), (evens[0][0] - odds[0][0], None)]
    found = [None] * (half + 1)
    found[0] = (evens[0][0] + odds[0][0], None)
    found[half] = (evens[0][0] - odds[0][0], None)
    found[half // 2] = (evens[half // 2][0], -odds[half // 2][0])
    for k in range(1, half // 2):
        cosine, sine = math.cos(2 * math.pi * k / count), -math.sin(2 * math.pi * k / count)
        (er, ei), (or_, oi) = evens[k], odds[k]
        tr, ti = cosine * or_ - sine * oi, cosine * oi + sine * or_
        found[k] = (er + tr, ei + ti)
        found[half - k] = (er - tr, ti - ei)
    return found


def real_inverse(modes):
    half = len(modes) - 1
    if half == 0:
        return [modes[0][0]]
    count = 2 * half
    if half == 1:
        return [modes[0][0] + modes[1][0], modes[0][0] - modes[1][0]]
    evens, odds = [None] * (half // 2 + 1), [None] * (half // 2 + 1)
    evens[0] = (modes[0][0] + modes[half][0], None)
    odds[0] = (modes[0][0] - modes[half][0], None)
    middle = modes[half // 2]
    evens[half // 2] = (2.0 * middle[0], None)
    odds[half // 2] = (-2.0 * middle[1], None)
    for k in range(1, half // 2):
        cosine, sine = math.cos(2 * math.pi * k / count), math.sin(2 * math.pi * k / count)
        (ar, ai), (br, bi) = modes[k], modes[half - k]
        dr, di = ar - br, ai + bi
        evens[k] = (ar + br, ai - bi)
        odds[k] = (cosine * dr - sine * di, cosine * di + sine * dr)
    first, second = real_inverse(evens), real_inverse(odds)
    return [part for pair in zip(first, second) for part in pair]


def pair_sum(value, distance):
    for axis in (-2, -1):
        dim = value.ndim + axis
        extent = value.shape[dim]
        upper = pltpu.roll(value, extent - distance, dim)
        lower = pltpu.roll(value, distance, dim)
        place = lax.broadcasted_iota(jnp.int32, value.shape, dim)
        value = value + jnp.where((place // distance) % 2 == 0, upper, lower)
    return value


def block_mean(value, distance):
    shape = (value.shape[0] // 2, 2) + value.shape[1:]
    paired = value.reshape(shape)
    return 0.125 * pair_sum(paired[:, 0] + paired[:, 1], distance)


def neighbour_weights(level, shape):
    spread, drifts = level_coefficients(level)
    distance = 2**level
    along_first = (drifts[0] - spread, -drifts[0] - spread)
    masked = []
    for dim in (0, 1):
        place = lax.broadcasted_iota(jnp.int32, shape, dim)
        upper = jnp.where(place < shape[dim] - distance, drifts[dim + 1] - spread, 0.0)
        lower = jnp.where(place >= distance, -drifts[dim + 1] - spread, 0.0)
        masked.append((upper, lower))
    return along_first, masked, distance


def neighbours(wide, weights):
    along_first, masked, distance = weights
    centre = wide[1:-1]
    total = along_first[0] * wide[2:] + along_first[1] * wide[:-2]
    for dim in (0, 1):
        extent = centre.shape[dim + 1]
        if distance >= extent:
            continue
        upper, lower = masked[dim]
        total = total + upper[None] * pltpu.roll(centre, extent - distance, dim + 1)
        total = total + lower[None] * pltpu.roll(centre, distance, dim + 1)
    return total


def blocks_of(extent, largest, body):
    block = min(extent, largest)

    def step(i, carry):
        body(pl.multiple_of(i * block, block), block)
        return carry

    if extent == block:
        body(0, block)
    else:
        lax.fori_loop(0, extent // block, step, 0)


BLOCK = 4


def prepare_level(level, caps, inverses, shifts):
    spread, unused = level_coefficients(level)
    s1, s2, s3 = shifts

    def body(start, block):
        cap = caps[level][pl.ds(start, block)]
        top, coupling, bottom = cap * s1 + 6.0 * spread, cap * s2, cap * s3 + 6.0 * spread
        scale = OMEGA / (top * bottom + coupling * coupling)
        inverses[level][pl.ds(start, block), 0] = bottom * scale
        inverses[level][pl.ds(start, block), 1] = coupling * scale
        inverses[level][pl.ds(start, block), 2] = top * scale
        if level + 1 < GRID_DEPTH:
            half = block // 2
            caps[level + 1][pl.ds(start // 2, half)] = block_mean(cap, 2**level)

    blocks_of(caps[level].shape[0], BLOCK, body)


def smooth_first(forcing, target, inverse):
    def body(start, block):
        here = pl.ds(start, block)
        a, b, c = inverse[here, 0], inverse[here, 1], inverse[here, 2]
        re, im = forcing[here, 0], forcing[here, 1]
        there = pl.ds(start + 1, block)
        target[there, 0] = a * re + b * im
        target[there, 1] = c * im - b * re

    blocks_of(forcing.shape[0], BLOCK, body)


def smooth(forcing, source, target, inverse, weights, offset=1, coarse=None):
    def body(start, block):
        here = pl.ds(start, block)
        wide_re = source[pl.ds(start, block + 2), 0]
        wide_im = source[pl.ds(start, block + 2), 1]
        r0 = forcing[here, 0] - neighbours(wide_re, weights)
        r1 = forcing[here, 1] - neighbours(wide_im, weights)
        a, b, c = inverse[here, 0], inverse[here, 1], inverse[here, 2]
        there = pl.ds(start + offset, block)
        target[there, 0] = (1.0 - OMEGA) * wide_re[1:-1] + (a * r0 + b * r1)
        target[there, 1] = (1.0 - OMEGA) * wide_im[1:-1] + (c * r1 - b * r0)

    blocks_of(forcing.shape[0], BLOCK, body)


def restrict_residual(level, forcing, source, cap, shifts, weights, target):
    spread, unused = level_coefficients(level)
    s1, s2, s3 = shifts

    def body(start, block):
        here = pl.ds(start, block)
        wide_re = source[pl.ds(start, block + 2), 0]
        wide_im = source[pl.ds(start, block + 2), 1]
        re, im = wide_re[1:-1], wide_im[1:-1]
        field = cap[here]
        r0 = forcing[here, 0] - neighbours(wide_re, weights)
        r1 = forcing[here, 1] - neighbours(wide_im, weights)
        r0 = r0 - (6.0 * spread * re + field * (s1 * re - s2 * im))
        r1 = r1 - (6.0 * spread * im + field * (s2 * re + s3 * im))
        half = pl.ds(start // 2, block // 2)
        target[half, 0] = block_mean(r0, 2**level)
        target[half, 1] = block_mean(r1, 2**level)

    blocks_of(forcing.shape[0], BLOCK, body)


def add_coarse(target, coarse):
    def body(start, block):
        half = block // 2
        for part in (0, 1):
            extra = coarse[pl.ds(start // 2 + 1, half), part]
            spread = jnp.broadcast_to(extra[:, None], (half, 2) + extra.shape[1:])
            there = pl.ds(start + 1, block)
            target[there, part] = target[there, part] + spread.reshape((block,) + extra.shape[1:])

    blocks_of(target.shape[0] - 2, BLOCK, body)


def cycle(level, forcings, caps, inverses, firsts, seconds, shifts, result):
    forcing, inverse = forcings[level], inverses[level]
    here, other = firsts[level], seconds[level]
    weights = neighbour_weights(level, forcing.shape[-2:])
    coarsest = level == GRID_DEPTH - 1
    smooth_first(forcing, here, inverse)
    for repeat in range((COARSE_SWEEPS if coarsest else SMOOTH) - 1):
        smooth(forcing, here, other, inverse, weights)
        here, other = other, here
    if coarsest:
        return here
    restrict_residual(level, forcing, here, caps[level], shifts, weights, forcings[level + 1])
    coarse = cycle(level + 1, forcings, caps, inverses, firsts, seconds, shifts, None)
    add_coarse(here, coarse)
    for repeat in range(SMOOTH):
        last = repeat == SMOOTH - 1 and result is not None
        target = result if last else other
        smooth(forcing, here, target, inverse, weights, offset=0 if last else 1)
        here, other = target, here
    return here


def whole_kernel(groups, slabs, shift_ref, residual_ref, capacity_ref, out_ref, *scratch):
    (series, spectrum, returned, values, result) = scratch[:5]
    depth = GRID_DEPTH
    forcings = scratch[5 : 5 + depth]
    caps = scratch[5 + depth : 5 + 2 * depth]
    inverses = scratch[5 + 2 * depth : 5 + 3 * depth]
    firsts = scratch[5 + 3 * depth : 5 + 4 * depth]
    seconds = scratch[5 + 4 * depth : 5 + 5 * depth]
    send1, recv1, send2, recv2, send3, recv3, send4, recv4, own, sendc, recvc = scratch[
        5 + 5 * depth :
    ]
    steps, thick = residual_ref.shape[:2]
    planes = thick // groups
    length = groups * steps
    devices = groups * slabs
    ratio_step = ALPHA_CORNER ** (1.0 / length)
    mine, slab = lax.axis_index("tm"), lax.axis_index("space")
    me = mine * slabs + slab
    base = slab * thick + mine * planes

    def peer_of(k):
        peer = lax.rem(me + k, devices)
        return peer, peer // slabs, lax.rem(peer, slabs)

    barrier = pltpu.get_barrier_semaphore()

    def greet(k, carry):
        unused, to_tm, to_space = peer_of(k)
        pl.semaphore_signal(barrier, inc=1, device_id=(to_tm, to_space), device_id_type=MESH)
        return carry

    lax.fori_loop(1, devices, greet, 0)
    for level in range(depth):
        for buffer in (firsts[level], seconds[level]):
            empty = jnp.zeros(buffer.shape[1:], jnp.float32)
            buffer[0] = empty
            buffer[buffer.shape[0] - 1] = empty
    pl.semaphore_wait(barrier, devices - 1)

    first_sends = []
    for p in range(planes):
        for d in range(1, groups):
            to_tm = lax.rem(mine + d, groups)
            copy = pltpu.make_async_remote_copy(
                src_ref=residual_ref.at[:, to_tm * planes + p],
                dst_ref=series.at[p, pl.ds(mine * steps, steps)],
                send_sem=send1.at[p, d],
                recv_sem=recv1.at[p, d],
                device_id=(to_tm, slab),
                device_id_type=MESH,
            )
            copy.start()
            first_sends.append(copy)
    own_steps = []
    for p in range(planes):
        copy = pltpu.make_async_copy(
            residual_ref.at[:, mine * planes + p],
            series.at[p, pl.ds(mine * steps, steps)],
            own.at[p],
        )
        copy.start()
        own_steps.append(copy)

    own_slab = pl.ds(slab * thick, thick)
    caps[0][own_slab] = capacity_ref[...]
    cap_sends = []
    for d in range(1, slabs // 2):
        copy = pltpu.make_async_remote_copy(
            src_ref=capacity_ref,
            dst_ref=caps[0].at[own_slab],
            send_sem=sendc.at[d],
            recv_sem=recvc.at[d],
            device_id=(mine, lax.rem(slab + 2 * d, slabs)),
            device_id_type=MESH,
        )
        copy.start()
        cap_sends.append(copy)
    parity = lax.rem(slab, 2)
    partner = slab + 1 - 2 * parity

    def forward_cap(d):
        index = lax.rem(slab + slabs - 2 * d, slabs)
        rows = pl.ds(index * thick, thick)
        copy = pltpu.make_async_remote_copy(
            src_ref=capacity_ref if d == 0 else caps[0].at[rows],
            dst_ref=caps[0].at[rows],
            send_sem=sendc.at[slabs // 2 + d],
            recv_sem=recvc.at[slabs // 2 + d],
            device_id=(mine, partner),
            device_id_type=MESH,
        )
        copy.start()
        return copy

    cap_forwards = [forward_cap(0)]

    def spread_mode(k, p):
        peer, to_tm, to_space = peer_of(k)
        return pltpu.make_async_remote_copy(
            src_ref=spectrum.at[p, peer],
            dst_ref=forcings[0].at[base + p],
            send_sem=send2.at[p],
            recv_sem=recv2.at[p],
            device_id=(to_tm, to_space),
            device_id_type=MESH,
        )

    own_modes = []
    for p in range(planes):
        own_steps[p].wait()
        for d in range(1, groups):
            first_sends[p * (groups - 1) + d - 1].wait_recv()
        modes = real_transform([ratio_step**t * series[p, t] for t in range(length)])
        spectrum[p, 0, 0] = modes[0][0]
        spectrum[p, 0, 1] = modes[length // 2][0]
        for k in range(1, length // 2):
            spectrum[p, k, 0] = modes[k][0]
            spectrum[p, k, 1] = modes[k][1]

        def start_mode(k, carry):
            spread_mode(k, p).start()
            return carry

        lax.fori_loop(1, devices, start_mode, 0)
        copy = pltpu.make_async_copy(
            spectrum.at[p, me], forcings[0].at[base + p], own.at[planes + p]
        )
        copy.start()
        own_modes.append(copy)
        if p == 0:
            for d in range(1, slabs // 2):
                cap_sends[d - 1].wait_recv()
                cap_forwards.append(forward_cap(d))

    for copy in cap_forwards:
        copy.wait_recv()
    shifts = tuple(shift_ref[me, j] for j in range(3))
    for level in range(depth):
        prepare_level(level, caps, inverses, shifts)

    def all_but_one(array, semaphore):
        part = array.at[pl.ds(0, devices - 1)]
        return pltpu.make_async_copy(part, part, semaphore)

    for p in range(planes):
        own_modes[p].wait()
        all_but_one(forcings[0], recv2.at[p]).wait()

    cycle(0, forcings, caps, inverses, firsts, seconds, shifts, result)

    def send_back(k, p):
        peer, to_tm, to_space = peer_of(k)
        return pltpu.make_async_remote_copy(
            src_ref=result.at[to_space * thick + to_tm * planes + p],
            dst_ref=returned.at[p, me],
            send_sem=send3.at[p],
            recv_sem=recv3.at[p],
            device_id=(to_tm, to_space),
            device_id_type=MESH,
        )

    own_back = []
    for p in range(planes):

        def start_back(k, carry):
            send_back(k, p).start()
            return carry

        lax.fori_loop(1, devices, start_back, 0)
        copy = pltpu.make_async_copy(
            result.at[base + p], returned.at[p, me], own.at[2 * planes + p]
        )
        copy.start()
        own_back.append(copy)

    last_copies = []
    for p in range(planes):
        own_back[p].wait()
        all_but_one(returned.at[p], recv3.at[p]).wait()
        modes = [(returned[p, 0, 0], None)]
        modes += [(returned[p, k, 0], returned[p, k, 1]) for k in range(1, length // 2)]
        modes += [(returned[p, 0, 1], None)]
        for t, value in enumerate(real_inverse(modes)):
            values[p, t] = value * (ratio_step**-t / length)
        for d in range(1, groups):
            to_tm = lax.rem(mine + d, groups)
            copy = pltpu.make_async_remote_copy(
                src_ref=values.at[p, pl.ds(to_tm * steps, steps)],
                dst_ref=out_ref.at[:, mine * planes + p],
                send_sem=send4.at[p, d],
                recv_sem=recv4.at[p, d],
                device_id=(to_tm, slab),
                device_id_type=MESH,
            )
            copy.start()
            last_copies.append(copy)
        out_ref[:, mine * planes + p] = values[p, pl.ds(mine * steps, steps)]

    for copy in last_copies:
        copy.wait()
    for copy in first_sends + cap_sends + cap_forwards:
        copy.wait_send()
    for p in range(planes):
        all_but_one(spectrum.at[p], send2.at[p]).wait()
        all_but_one(result, send3.at[p]).wait()


def fused(groups, slabs, residual, capacity):
    steps, thick, second, third = residual.shape
    length, devices = groups * steps, groups * slabs
    planes, extent = thick // groups, slabs * thick
    tile = (second, third)
    ratio_step = ALPHA_CORNER ** (1.0 / length)
    angle = 2.0 * np.pi / length * np.arange(devices)
    table = np.stack(
        [
            (1.0 - ratio_step * np.cos(angle)) / STEP_SIZE,
            ratio_step * np.sin(angle) / STEP_SIZE,
            (1.0 - ratio_step * np.cos(angle)) / STEP_SIZE,
        ],
        axis=1,
    )
    table[0, 1], table[0, 2] = 0.0, (1.0 + ratio_step) / STEP_SIZE
    extents = [extent // 2**level for level in range(GRID_DEPTH)]
    vmem = lambda *shape: pltpu.VMEM(shape + tile, jnp.float32)
    sems = lambda *shape: pltpu.SemaphoreType.DMA(shape)
    scratch = [
        vmem(planes, length),
        vmem(planes, devices, 2),
        vmem(planes, devices, 2),
        vmem(planes, length),
        vmem(extent, 2),
        *[vmem(n, 2) for n in extents],
        *[vmem(n) for n in extents],
        *[vmem(n, 3) for n in extents],
        *[vmem(n + 2, 2) for n in extents],
        *[vmem(n + 2, 2) for n in extents],
        sems(planes, groups),
        sems(planes, groups),
        sems(planes),
        sems(planes),
        sems(planes),
        sems(planes),
        sems(planes, groups),
        sems(planes, groups),
        sems(3 * planes),
        sems(slabs),
        sems(slabs),
    ]
    return pl.pallas_call(
        functools.partial(whole_kernel, groups, slabs),
        out_shape=jax.ShapeDtypeStruct(residual.shape, jnp.float32),
        in_specs=[
            pl.BlockSpec(memory_space=pltpu.SMEM),
            pl.BlockSpec(memory_space=pltpu.VMEM),
            pl.BlockSpec(memory_space=pltpu.VMEM),
        ],
        out_specs=pl.BlockSpec(memory_space=pltpu.VMEM),
        scratch_shapes=scratch,
        compiler_params=pltpu.CompilerParams(
            collective_id=0, has_side_effects=True, vmem_limit_bytes=32 * 2**20
        ),
    )(jnp.asarray(table, jnp.float32), residual, capacity)


def fits_fused(groups, slabs, residual):
    steps, thick, second, third = residual.shape
    length = groups * steps
    power = length & (length - 1) == 0
    return (
        power
        and groups * slabs == length // 2
        and slabs % 2 == 0
        and thick % groups == 0
        and (slabs * thick) % (BLOCK * 2 ** (GRID_DEPTH - 1)) == 0
        and (second, third) == (8, 128)
    )


def either(residual, capacity):
    groups, slabs = lax.axis_size("tm"), lax.axis_size("space")
    if fits_fused(groups, slabs, residual):
        return fused(groups, slabs, residual, capacity)
    return on_device(residual, capacity)


def solution(mesh):
    return jax.shard_map(
        either,
        mesh=mesh,
        in_specs=(P("tm", "space", None, None), P("space", None, None)),
        out_specs=P("tm", "space", None, None),
        check_vma=False,
    )
```

profile of v0, /device:TPU:0, one launch (start us, length us, event | category | flops | bytes accessed | tf_op | source)
XLA Modules:
  0.0 62.1 jit_solution(7546712430721895442)
XLA Ops:
  0.0 0.0 copy-start
  0.0 1.0 %copy-done = f32[16,8,8,128]{3,2,1,0:T(8,128)S(1)} copy-done((f32[16,8,8,128]{3,2,1,0:T(8,128)S(1)}, f32[16,8,8,128]{3,2,1,0:T(8,128)}, u32[]{:S(2)}) %copy-start) | copy-done | bytes 524312
  1.0 0.0 copy-start.1
  1.0 0.8 %copy-done.1 = f32[8,8,128]{2,1,0:T(8,128)S(1)} copy-done((f32[8,8,128]{2,1,0:T(8,128)S(1)}, f32[8,8,128]{2,1,0:T(8,128)}, u32[]{:S(2)}) %copy-start.1) | copy-done | bytes 32792
  1.8 0.0 copy-start.2
  1.8 0.7 %copy-done.2 = f32[32,3]{1,0:T(8,128)S(1)} copy-done((f32[32,3]{1,0:T(8,128)S(1)}, f32[32,3]{1,0:T(8,128)}, u32[]{:S(2)}) %copy-start.2) | copy-done | bytes 408
  2.5 58.7 %shard_map.37 = f32[16,8,8,128]{3,2,1,0:T(8,128)S(1)} custom-call(f32[32,3]{1,0:T(8,128)S(1)} %copy-done.2, f32[16,8,8,128]{3,2,1,0:T(8,128)S(1)} %copy-done, f32[8,8,128]{2,1,0:T(8,128)S(1)} %copy-done.1), custom_call_target="tpu_custom_call" | custom-call | tf_op jit(solution)/shard_map/pallas_call | solution.py:707
  61.3 0.8 %copy.5 = f32[16,8,8,128]{3,2,1,0:T(8,128)} copy(f32[16,8,8,128]{3,2,1,0:T(8,128)S(1)} %shard_map.37) | data formatting | bytes 1048576
Async XLA Ops:
  0.0 1.0 %copy-start = (f32[16,8,8,128]{3,2,1,0:T(8,128)S(1)}, f32[16,8,8,128]{3,2,1,0:T(8,128)}, u32[]{:S(2)}) copy-start(f32[16,8,8,128]{3,2,1,0:T(8,128)} %residual_ref.1) | copy-start | bytes 1572868
  1.0 0.8 %copy-start.1 = (f32[8,8,128]{2,1,0:T(8,128)S(1)}, f32[8,8,128]{2,1,0:T(8,128)}, u32[]{:S(2)}) copy-start(f32[8,8,128]{2,1,0:T(8,128)} %capacity_ref.1) | copy-start | bytes 98308
  1.8 0.7 %copy-start.2 = (f32[32,3]{1,0:T(8,128)S(1)}, f32[32,3]{1,0:T(8,128)}, u32[]{:S(2)}) copy-start(f32[32,3]{1,0:T(8,128)} %constant.2.clone.shift_ref) | copy-start | bytes 1156
where the time goes:
time: 62.3 us; the launch traced here: 62.1 us
  Pallas kernels  58.7 us (94%)
  local copies, waits for them, and re-layouts  3.31 us (5%)
    pallas_call x1, Pallas kernels, fused(): pl.pallas_call(functools.partial(whole_kernel, groups, slabs), out_shape=...  58.7 us
    unnamed x7, local copies, waits for them, and re-layouts  3.31 us

commit v1 on v0

--- a/solution.py
+++ b/solution.py
@@ -352,7 +352,7 @@
         lax.fori_loop(0, extent // block, step, 0)
 
 
-BLOCK = 4
+BLOCK = 32
 
 
 def prepare_level(level, caps, inverses, shifts):
@@ -455,15 +455,17 @@
     return here
 
 
-def whole_kernel(groups, slabs, shift_ref, residual_ref, capacity_ref, out_ref, *scratch):
+def whole_kernel(groups, slabs, shift_table, residual_hbm, capacity_hbm, out_ref, *scratch):
     (series, spectrum, returned, values, result) = scratch[:5]
+    residual_ref = scratch[-1]
+    scratch = scratch[:-1]
     depth = GRID_DEPTH
     forcings = scratch[5 : 5 + depth]
     caps = scratch[5 + depth : 5 + 2 * depth]
     inverses = scratch[5 + 2 * depth : 5 + 3 * depth]
     firsts = scratch[5 + 3 * depth : 5 + 4 * depth]
     seconds = scratch[5 + 4 * depth : 5 + 5 * depth]
-    send1, recv1, send2, recv2, send3, recv3, send4, recv4, own, sendc, recvc = scratch[
+    send1, recv1, send2, recv2, send3, recv3, send4, recv4, own, sendc, recvc, ready = scratch[
         5 + 5 * depth :
     ]
     steps, thick = residual_ref.shape[:2]
@@ -476,23 +478,45 @@
     base = slab * thick + mine * planes
 
     def peer_of(k):
-        peer = lax.rem(me + k, devices)
-        return peer, peer // slabs, lax.rem(peer, slabs)
-
+        to_tm = lax.rem(mine + k, groups)
+        to_space = lax.rem(slab + k // groups, slabs)
+        return to_tm * slabs + to_space, to_tm, to_space
+
+    own_slab = pl.ds(slab * thick, thick)
+    take_residual = pltpu.make_async_copy(residual_hbm, residual_ref, own.at[3 * planes])
+    take_capacity = pltpu.make_async_copy(
+        capacity_hbm, caps[0].at[own_slab], own.at[3 * planes + 1]
+    )
+    take_residual.start()
+    take_capacity.start()
     barrier = pltpu.get_barrier_semaphore()
 
-    def greet(k, carry):
-        unused, to_tm, to_space = peer_of(k)
-        pl.semaphore_signal(barrier, inc=1, device_id=(to_tm, to_space), device_id_type=MESH)
-        return carry
-
-    lax.fori_loop(1, devices, greet, 0)
+    partner = slab + 1 - 2 * lax.rem(slab, 2)
+    below, above = slab >= 2, slab < slabs - 2
+    sides = jnp.where(below, 1, 0) + jnp.where(above, 1, 0)
+
+    def tell_sides(semaphore):
+        for there, step in ((below, -2), (above, 2)):
+
+            @pl.when(there)
+            def _():
+                pl.semaphore_signal(
+                    semaphore, inc=1, device_id=(mine, slab + step), device_id_type=MESH
+                )
+
+    for d in range(1, groups):
+        pl.semaphore_signal(
+            barrier, inc=1, device_id=(lax.rem(mine + d, groups), slab), device_id_type=MESH
+        )
+    tell_sides(barrier)
+    pl.semaphore_signal(barrier, inc=1, device_id=(mine, partner), device_id_type=MESH)
     for level in range(depth):
         for buffer in (firsts[level], seconds[level]):
             empty = jnp.zeros(buffer.shape[1:], jnp.float32)
             buffer[0] = empty
             buffer[buffer.shape[0] - 1] = empty
-    pl.semaphore_wait(barrier, devices - 1)
+    take_residual.wait()
+    pl.semaphore_wait(barrier, groups + sides)
 
     first_sends = []
     for p in range(planes):
@@ -518,12 +542,18 @@
         copy.start()
         own_steps.append(copy)
 
-    own_slab = pl.ds(slab * thick, thick)
-    caps[0][own_slab] = capacity_ref[...]
+    for turn in range(slabs // 2 - 1):
+        tell_sides(ready.at[turn])
+        pl.semaphore_wait(ready.at[turn], sides)
+    last = slabs // 2 - 1
+    pl.semaphore_signal(ready.at[last], inc=1, device_id=(mine, partner), device_id_type=MESH)
+    pl.semaphore_wait(ready.at[last], 1)
+
+    take_capacity.wait()
     cap_sends = []
     for d in range(1, slabs // 2):
         copy = pltpu.make_async_remote_copy(
-            src_ref=capacity_ref,
+            src_ref=caps[0].at[own_slab],
             dst_ref=caps[0].at[own_slab],
             send_sem=sendc.at[d],
             recv_sem=recvc.at[d],
@@ -532,14 +562,12 @@
         )
         copy.start()
         cap_sends.append(copy)
-    parity = lax.rem(slab, 2)
-    partner = slab + 1 - 2 * parity
 
     def forward_cap(d):
         index = lax.rem(slab + slabs - 2 * d, slabs)
         rows = pl.ds(index * thick, thick)
         copy = pltpu.make_async_remote_copy(
-            src_ref=capacity_ref if d == 0 else caps[0].at[rows],
+            src_ref=caps[0].at[rows],
             dst_ref=caps[0].at[rows],
             send_sem=sendc.at[slabs // 2 + d],
             recv_sem=recvc.at[slabs // 2 + d],
@@ -591,7 +619,12 @@
 
     for copy in cap_forwards:
         copy.wait_recv()
-    shifts = tuple(shift_ref[me, j] for j in range(3))
+    shifts = []
+    for column in range(3):
+        value = jnp.float32(shift_table[0, column])
+        for k in range(1, devices):
+            value = jnp.where(me == k, jnp.float32(shift_table[k, column]), value)
+        shifts.append(value)
     for level in range(depth):
         prepare_level(level, caps, inverses, shifts)
 
@@ -662,6 +695,10 @@
         all_but_one(result, send3.at[p]).wait()
 
 
+def level_extents(extent):
+    return [extent // 2**level for level in range(GRID_DEPTH)]
+
+
 def fused(groups, slabs, residual, capacity):
     steps, thick, second, third = residual.shape
     length, devices = groups * steps, groups * slabs
@@ -678,7 +715,7 @@
         axis=1,
     )
     table[0, 1], table[0, 2] = 0.0, (1.0 + ratio_step) / STEP_SIZE
-    extents = [extent // 2**level for level in range(GRID_DEPTH)]
+    extents = level_extents(extent)
     vmem = lambda *shape: pltpu.VMEM(shape + tile, jnp.float32)
     sems = lambda *shape: pltpu.SemaphoreType.DMA(shape)
     scratch = [
@@ -700,24 +737,25 @@
         sems(planes),
         sems(planes, groups),
         sems(planes, groups),
-        sems(3 * planes),
+        sems(3 * planes + 2),
         sems(slabs),
         sems(slabs),
+        pltpu.SemaphoreType.REGULAR((slabs // 2,)),
+        pltpu.VMEM(residual.shape, jnp.float32),
     ]
     return pl.pallas_call(
-        functools.partial(whole_kernel, groups, slabs),
+        functools.partial(whole_kernel, groups, slabs, table),
         out_shape=jax.ShapeDtypeStruct(residual.shape, jnp.float32),
         in_specs=[
-            pl.BlockSpec(memory_space=pltpu.SMEM),
-            pl.BlockSpec(memory_space=pltpu.VMEM),
-            pl.BlockSpec(memory_space=pltpu.VMEM),
+            pl.BlockSpec(memory_space=pltpu.HBM),
+            pl.BlockSpec(memory_space=pltpu.HBM),
         ],
         out_specs=pl.BlockSpec(memory_space=pltpu.VMEM),
         scratch_shapes=scratch,
         compiler_params=pltpu.CompilerParams(
             collective_id=0, has_side_effects=True, vmem_limit_bytes=32 * 2**20
         ),
-    )(jnp.asarray(table, jnp.float32), residual, capacity)
+    )(residual, capacity)
 
 
 def fits_fused(groups, slabs, residual):
@@ -729,7 +767,7 @@
         and groups * slabs == length // 2
         and slabs % 2 == 0
         and thick % groups == 0
-        and (slabs * thick) % (BLOCK * 2 ** (GRID_DEPTH - 1)) == 0
+        and all(n % 2 == 0 and n % min(n, BLOCK) == 0 for n in level_extents(slabs * thick))
         and (second, third) == (8, 128)
     )
 

time: 62.3 us -> 49.6 us (0.80)
  Pallas kernels: 58.7 us -> 46.8 us
  local copies, waits for them, and re-layouts: 3.31 us -> 2.59 us
    pallas_call x1, Pallas kernels: 58.7 us -> 46.8 us  [fused(): pl.pallas_call(functools.partial(whole_kernel, groups, slabs, table), out...]
    unnamed x7 -> x5, local copies, waits for them, and re-layouts: 3.31 us -> 2.59 us
where the time goes in v1:
time: 49.6 us; the launch traced here: 49.4 us
  Pallas kernels  46.8 us (94%)
  local copies, waits for them, and re-layouts  2.59 us (5%)
    pallas_call x1, Pallas kernels, fused(): pl.pallas_call(functools.partial(whole_kernel, groups, slabs, table), out...  46.8 us
    unnamed x5, local copies, waits for them, and re-layouts  2.59 us

profile of v1, /device:TPU:0, one launch (start us, length us, event | category | flops | bytes accessed | tf_op | source)
XLA Modules:
  0.0 49.4 jit_solution(13253216506955605713)
XLA Ops:
  0.0 0.0 copy-start
  0.0 1.0 %copy-done = f32[16,8,8,128]{3,2,1,0:T(8,128)S(1)} copy-done((f32[16,8,8,128]{3,2,1,0:T(8,128)S(1)}, f32[16,8,8,128]{3,2,1,0:T(8,128)}, u32[]{:S(2)}) %copy-start) | copy-done | bytes 524312
  1.0 0.0 copy-start.1
  1.0 0.8 %copy-done.1 = f32[8,8,128]{2,1,0:T(8,128)S(1)} copy-done((f32[8,8,128]{2,1,0:T(8,128)S(1)}, f32[8,8,128]{2,1,0:T(8,128)}, u32[]{:S(2)}) %copy-start.1) | copy-done | bytes 32792
  1.8 46.8 %shard_map.28 = f32[16,8,8,128]{3,2,1,0:T(8,128)S(1)} custom-call(f32[16,8,8,128]{3,2,1,0:T(8,128)S(1)} %copy-done, f32[8,8,128]{2,1,0:T(8,128)S(1)} %copy-done.1), custom_call_target="tpu_custom_call" | custom-call | tf_op jit(solution)/shard_map/pallas_call | solution.py:746
  48.6 0.8 %copy.4 = f32[16,8,8,128]{3,2,1,0:T(8,128)} copy(f32[16,8,8,128]{3,2,1,0:T(8,128)S(1)} %shard_map.28) | data formatting | bytes 1048576
Async XLA Ops:
  0.0 1.0 %copy-start = (f32[16,8,8,128]{3,2,1,0:T(8,128)S(1)}, f32[16,8,8,128]{3,2,1,0:T(8,128)}, u32[]{:S(2)}) copy-start(f32[16,8,8,128]{3,2,1,0:T(8,128)} %residual_hbm.1) | copy-start | bytes 1572868
  1.0 0.8 %copy-start.1 = (f32[8,8,128]{2,1,0:T(8,128)S(1)}, f32[8,8,128]{2,1,0:T(8,128)}, u32[]{:S(2)}) copy-start(f32[8,8,128]{2,1,0:T(8,128)} %capacity_hbm.1) | copy-start | bytes 98308

commit v2 on v1

--- a/solution.py
+++ b/solution.py
@@ -352,7 +352,7 @@
         lax.fori_loop(0, extent // block, step, 0)
 
 
-BLOCK = 32
+BLOCK = 64
 
 
 def prepare_level(level, caps, inverses, shifts):
@@ -612,11 +612,10 @@
         )
         copy.start()
         own_modes.append(copy)
-        if p == 0:
-            for d in range(1, slabs // 2):
-                cap_sends[d - 1].wait_recv()
-                cap_forwards.append(forward_cap(d))
-
+
+    for d in range(1, slabs // 2):
+        cap_sends[d - 1].wait_recv()
+        cap_forwards.append(forward_cap(d))
     for copy in cap_forwards:
         copy.wait_recv()
     shifts = []

time: 49.6 us -> 49.3 us (level)
  no operation moved by 1% of the time
where the time goes in v2:
time: 49.3 us; the launch traced here: 49 us
  Pallas kernels  46.4 us (94%)
  local copies, waits for them, and re-layouts  2.59 us (5%)
    pallas_call x1, Pallas kernels, fused(): pl.pallas_call(functools.partial(whole_kernel, groups, slabs, table), out...  46.4 us
    unnamed x5, local copies, waits for them, and re-layouts  2.59 us

profile of v2, /device:TPU:0, one launch (start us, length us, event | category | flops | bytes accessed | tf_op | source)
XLA Modules:
  0.0 49.0 jit_solution(4270941216031411824)
XLA Ops:
  0.0 0.0 copy-start
  0.0 1.0 %copy-done = f32[16,8,8,128]{3,2,1,0:T(8,128)S(1)} copy-done((f32[16,8,8,128]{3,2,1,0:T(8,128)S(1)}, f32[16,8,8,128]{3,2,1,0:T(8,128)}, u32[]{:S(2)}) %copy-start) | copy-done | bytes 524312
  1.0 0.0 copy-start.1
  1.0 0.8 %copy-done.1 = f32[8,8,128]{2,1,0:T(8,128)S(1)} copy-done((f32[8,8,128]{2,1,0:T(8,128)S(1)}, f32[8,8,128]{2,1,0:T(8,128)}, u32[]{:S(2)}) %copy-start.1) | copy-done | bytes 32792
  1.8 46.4 %shard_map.28 = f32[16,8,8,128]{3,2,1,0:T(8,128)S(1)} custom-call(f32[16,8,8,128]{3,2,1,0:T(8,128)S(1)} %copy-done, f32[8,8,128]{2,1,0:T(8,128)S(1)} %copy-done.1), custom_call_target="tpu_custom_call" | custom-call | tf_op jit(solution)/shard_map/pallas_call | solution.py:745
  48.2 0.8 %copy.4 = f32[16,8,8,128]{3,2,1,0:T(8,128)} copy(f32[16,8,8,128]{3,2,1,0:T(8,128)S(1)} %shard_map.28) | data formatting | bytes 1048576
Async XLA Ops:
  0.0 1.0 %copy-start = (f32[16,8,8,128]{3,2,1,0:T(8,128)S(1)}, f32[16,8,8,128]{3,2,1,0:T(8,128)}, u32[]{:S(2)}) copy-start(f32[16,8,8,128]{3,2,1,0:T(8,128)} %residual_hbm.1) | copy-start | bytes 1572868
  1.0 0.8 %copy-start.1 = (f32[8,8,128]{2,1,0:T(8,128)S(1)}, f32[8,8,128]{2,1,0:T(8,128)}, u32[]{:S(2)}) copy-start(f32[8,8,128]{2,1,0:T(8,128)} %capacity_hbm.1) | copy-start | bytes 98308
